TPU v7x, 256 devices: a whole 4x4x8 slice. The times are simulated.
256 devices in a mesh: gx: 4 (over x), gy: 4 (over y), gz: 16 (over z, core).
Axes of the slice: x: 4, y: 4, z: 8, core: 2. Of those that a mesh axis runs over, the one named last changes fastest.
Arguments:
- densities: float32 [7, 512, 128, 512], P(None, 'gz', 'gy', 'gx'), may hold values from -6 to 6
- residuals: float32 [7, 512, 128, 512], P(None, 'gz', 'gy', 'gx'), may hold values from -320 to 320
Outputs:
- new_density: float32 [512, 128, 512], P('gz', 'gy', 'gx')
- weights: float32 [7], replicated
All inputs are finite; a program needn't handle non-finite values.
Results may differ from a plain program's by a relative error of at most 0.000087.
Values sent between devices are 32-bit elements; how exact they have to be, the bound alone decides.
A program may use at most 64 MiB of HBM per device.

v0:
```python
import math
import jax
import jax.numpy as jnp
from jax import lax
from jax.sharding import Mesh
from jax.sharding import PartitionSpec as P

SWEEPS = 3
GX_GY_GZ = ("gx", "gy", "gz_0", "gz_1")
GZ = ("gz_0", "gz_1")
shift_value = 0.15
mix_amount = 0.7


def extended(cells, sides, width):
    for axis, dim in sides:
        count = lax.axis_size(axis)
        head = lax.slice_in_dim(cells, 0, width, axis=dim)
        tail = lax.slice_in_dim(cells, cells.shape[dim] - width, cells.shape[dim], axis=dim)
        cells = jnp.concatenate(
            [
                lax.ppermute(tail, axis, [(i, (i + 1) % count) for i in range(count)]),
                cells,
                lax.ppermute(head, axis, [((i + 1) % count, i) for i in range(count)]),
            ],
            axis=dim,
        )
    return cells


def one_axis_at_a_time(shard, axes):
    for axis in axes:
        shard = lax.psum(shard, axis)
    return shard


def sweep_weights():
    diag_value = 6.0 + shift_value
    upper = (shift_value + 12.0) / diag_value
    lower = upper / 3.0
    return [
        1.0
        / (
            (upper + lower) / 2.0
            + (upper - lower) / 2.0 * math.cos(math.pi * (2 * k - 1) / (2 * SWEEPS))
        )
        for k in range(1, SWEEPS + 1)
    ]


def neighbours(padded):
    total = padded[:, 2:, 1:-1, 1:-1] + padded[:, :-2, 1:-1, 1:-1]
    total = total + padded[:, 1:-1, 2:, 1:-1] + padded[:, 1:-1, :-2, 1:-1]
    return total + padded[:, 1:-1, 1:-1, 2:] + padded[:, 1:-1, 1:-1, :-2]


def shrink(field):
    return field[:, 1:-1, 1:-1, 1:-1]


def relax(padded, rhs, omega):
    diag_value = 6.0 + shift_value
    centre = shrink(padded)
    return centre + omega * (rhs - diag_value * centre + neighbours(padded)) / diag_value


def precondition(fields):
    diag_value = 6.0 + shift_value
    omegas = sweep_weights()
    padded = extended(fields, (("gx", 3), ("gy", 2), (GZ, 1)), SWEEPS)
    rhs = 6.0 * shrink(padded) - neighbours(padded)
    iterate = omegas[0] * rhs / diag_value
    for position in range(1, SWEEPS):
        rhs = shrink(rhs)
        iterate = relax(iterate, rhs, omegas[position])
    return iterate


def on_device(densities, residuals):
    count = residuals.shape[0]
    flat = residuals.reshape(count, -1)
    local = jnp.dot(
        flat, flat.T, precision=lax.Precision.HIGHEST, preferred_element_type=jnp.float32
    )
    gram = one_axis_at_a_time(local, GX_GY_GZ)
    factor = jnp.linalg.cholesky(gram)
    ones_column = jnp.ones((count, 1), jnp.float32)
    middle = lax.linalg.triangular_solve(factor, ones_column, left_side=True, lower=True)
    solved = lax.linalg.triangular_solve(
        factor, middle, left_side=True, lower=True, transpose_a=True
    )[:, 0]
    weights = solved / jnp.sum(solved)
    blended = jnp.tensordot(weights, densities, axes=1, precision=lax.Precision.HIGHEST)
    combined = jnp.tensordot(weights, residuals, axes=1, precision=lax.Precision.HIGHEST)
    update = precondition(combined[None])[0]
    return (blended + mix_amount * update, weights)


def solution(mesh):
    torus = Mesh(
        mesh.devices.reshape(mesh.shape["gx"], mesh.shape["gy"], 8, 2), ("gx", "gy", "gz_0", "gz_1")
    )
    return jax.shard_map(
        on_device,
        mesh=torus,
        in_specs=(P(None, GZ, "gy", "gx"), P(None, GZ, "gy", "gx")),
        out_specs=(P(GZ, "gy", "gx"), P()),
        check_vma=False,
    )
```

profile of v0, /device:TPU:30, one launch (start us, length us, event | category | flops | bytes accessed | tf_op | source)
XLA Modules:
  0.0 109.0 jit_solution(10908965110666886729)
XLA Ops:
  0.6 14.5 %fusion.10 = f32[7,7]{0,1:T(8,128)S(1)} fusion(f32[7,32,32,128]{3,2,1,0:T(8,128)} %param.3), kind=kOutput, calls=%fused_computation.23 | convolution fusion | flops 77070336 | bytes 3670212 | tf_op jit(solution)/shard_map/dot_general | solution.py:82
  15.1 7.5 %psum.28 = f32[7,7]{0,1:T(8,128)S(1)} all-reduce(f32[7,7]{0,1:T(8,128)S(1)} %fusion.10), channel_id=1, replica_groups=mesh['gx'=4,'gy'=4,'gz_0'=8,'gz_1'=2] {'gx'}, use_global_device_ids=true, to_apply=%region_0.0 | all-reduce | flops 49 | bytes 392 | tf_op jit(solution)/shard_map/psum | solution.py:33
  22.6 8.0 %psum.29 = f32[7,7]{0,1:T(8,128)S(1)} all-reduce(f32[7,7]{0,1:T(8,128)S(1)} %psum.28), channel_id=1, replica_groups=mesh['gx'=4,'gy'=4,'gz_0'=8,'gz_1'=2] {'gy'}, use_global_device_ids=true, to_apply=%region_1.0 | all-reduce | flops 49 | bytes 392 | tf_op jit(solution)/shard_map/psum | solution.py:33
  30.5 19.5 %psum.30 = f32[7,7]{0,1:T(8,128)S(1)} all-reduce(f32[7,7]{0,1:T(8,128)S(1)} %psum.29), channel_id=1, replica_groups=mesh['gx'=4,'gy'=4,'gz_0'=8,'gz_1'=2] {'gz_0'}, use_global_device_ids=true, to_apply=%region_2.0 | all-reduce | flops 49 | bytes 392 | tf_op jit(solution)/shard_map/psum | solution.py:33
  50.0 2.5 %psum.31 = f32[7,7]{0,1:T(8,128)S(1)} all-reduce(f32[7,7]{0,1:T(8,128)S(1)} %psum.30), channel_id=1, replica_groups=mesh['gx'=4,'gy'=4,'gz_0'=8,'gz_1'=2] {'gz_1'}, use_global_device_ids=true, to_apply=%region_3.0 | all-reduce | flops 49 | bytes 392 | tf_op jit(solution)/shard_map/psum | solution.py:33
  52.6 0.6 cholesky.16
  53.2 0.6 compare_reduce_fusion
  53.9 0.6 fusion.19
  54.6 0.5 custom-call.8
  55.2 0.8 fusion.29
  56.0 0.6 broadcast_divide_fusion
  56.6 7.8 %fusion = f32[1,32,32,128]{3,0,2,1:T(1,128)S(1)} fusion(f32[7,32,32,128]{3,2,1,0:T(8,128)} %param.3, f32[7]{0:T(128)S(1)} %broadcast_divide_fusion), kind=kOutput, calls=%fused_computation | convolution fusion | flops 11010048 | bytes 4194332 | tf_op jit(solution)/shard_map/dot_general | solution.py:94
  64.7 3.6 %collective-permute-start = (f32[1,32,32,3]{3,2,1,0:T(8,128)S(1)}, f32[1,32,32,3]{3,2,1,0:T(8,128)S(1)}, u32[]{:S(2)}, u32[]{:S(2)}) collective-permute-start(f32[1,32,32,3]{3,2,1,0:T(8,128)S(1)} %get-tuple-element.8), channel_id=1, source_target_pairs={{0,64},{64,128},{128,192},{192,0},{1,65},{65,129},{129,193},{193,1... | collective-permute-start | bytes 36872 | tf_op jit(solution)/shard_map/ppermute | solution.py:22
  68.3 11.5 %collective-permute-done = f32[1,32,32,3]{3,2,1,0:T(8,128)S(1)} collective-permute-done((f32[1,32,32,3]{3,2,1,0:T(8,128)S(1)}, f32[1,32,32,3]{3,2,1,0:T(8,128)S(1)}, u32[]{:S(2)}, u32[]{:S(2)}) %collective-permute-start) | collective-permute-done | bytes 12320 | tf_op jit(solution)/shard_map/ppermute | solution.py:22
  79.8 3.4 %collective-permute-done.1 = f32[1,32,32,3]{3,2,1,0:T(8,128)S(1)} collective-permute-done((f32[1,32,32,3]{3,2,1,0:T(8,128)S(1)}, f32[1,32,32,3]{3,2,1,0:T(8,128)S(1)}, u32[]{:S(2)}, u32[]{:S(2)}) %collective-permute-start.1) | collective-permute-done | bytes 12320 | tf_op jit(solution)/shard_map/ppermute | solution.py:24
  83.5 3.6 %collective-permute-start.2 = (f32[1,32,3,134]{3,2,1,0:T(4,128)S(1)}, f32[1,32,3,134]{3,2,1,0:T(4,128)S(1)}, u32[]{:S(2)}, u32[]{:S(2)}) collective-permute-start(f32[1,32,3,134]{3,2,1,0:T(4,128)S(1)} %get-tuple-element.6), channel_id=1, source_target_pairs={{0,16},{16,32},{32,48},{48,0},{1,17},{17,33},{33,49},{49,1},{2,18}... | collective-permute-start | bytes 154376 | tf_op jit(solution)/shard_map/ppermute | solution.py:22
  87.1 2.5 %collective-permute-done.2 = f32[1,32,3,134]{3,2,1,0:T(4,128)S(1)} collective-permute-done((f32[1,32,3,134]{3,2,1,0:T(4,128)S(1)}, f32[1,32,3,134]{3,2,1,0:T(4,128)S(1)}, u32[]{:S(2)}, u32[]{:S(2)}) %collective-permute-start.2) | collective-permute-done | bytes 51488 | tf_op jit(solution)/shard_map/ppermute | solution.py:22
  89.6 3.7 %collective-permute-done.3 = f32[1,32,3,134]{3,2,1,0:T(4,128)S(1)} collective-permute-done((f32[1,32,3,134]{3,2,1,0:T(4,128)S(1)}, f32[1,32,3,134]{3,2,1,0:T(4,128)S(1)}, u32[]{:S(2)}, u32[]{:S(2)}) %collective-permute-start.3) | collective-permute-done | bytes 51488 | tf_op jit(solution)/shard_map/ppermute | solution.py:24
  93.5 2.9 %collective-permute-start.5 = (f32[1,3,38,134]{3,2,1,0:T(8,128)S(1)}, f32[1,3,38,134]{3,2,1,0:T(8,128)S(1)}, u32[]{:S(2)}, u32[]{:S(2)}) collective-permute-start(f32[1,3,38,134]{3,2,1,0:T(8,128)S(1)} %get-tuple-element.5), channel_id=1, source_target_pairs={{1,0},{2,1},{3,2},{4,3},{5,4},{6,5},{7,6},{8,7},{9,8},{10,9},{11,1... | collective-permute-start | bytes 183320 | tf_op jit(solution)/shard_map/ppermute | solution.py:24
  96.4 5.2 %fusion.4 = f32[1,32,32,128]{3,0,2,1:T(1,128)S(1)} fusion(f32[7,32,32,128]{3,2,1,0:T(8,128)S(1)} %copy-done, f32[7]{0:T(128)S(1)} %broadcast_divide_fusion), kind=kOutput, calls=%fused_computation.4 | convolution fusion | flops 11010048 | bytes 4194332 | tf_op jit(solution)/shard_map/dot_general | solution.py:93
  101.6 0.6 pad_maximum_fusion
  102.2 2.3 %broadcast_multiply_fusion = (f32[1,36,36,132]{3,2,1,0:T(8,128)S(1)}, f32[1,36,36,132]{3,2,1,0:T(8,128)S(1)}) fusion(f32[1,38,38,134]{3,2,1,0:T(8,128)S(1)} %pad_maximum_fusion), kind=kLoop, calls=%fused_computation.26 | loop fusion | flops 1368576 | bytes 6158592 | tf_op jit(solution)/shard_map/div | solution.py:72
  104.6 2.6 %fusion.9 = f32[1,34,34,130]{3,2,1,0:T(8,128)S(1)} fusion(f32[1,36,36,132]{3,2,1,0:T(8,128)S(1)} %get-tuple-element.2, f32[1,36,36,132]{3,2,1,0:T(8,128)S(1)} %get-tuple-element.3), kind=kLoop, calls=%fused_computation.17 | loop fusion | flops 1502800 | bytes 5410080 | tf_op jit(solution)/shard_map/add | solution.py:64
  107.2 1.8 %fusion.18 = f32[32,32,128]{2,1,0:T(8,128)} fusion(f32[32,32,128]{2,1,0:T(8,128)S(1)} %bitcast.45, f32[1,34,34,130]{3,2,1,0:T(8,128)S(1)} %fusion.9, f32[1,36,36,132]{3,2,1,0:T(8,128)S(1)} %get-tuple-element.3), kind=kLoop, calls=%fused_computation.33 | loop fusion | flops 1572864 | bytes 5242880 | tf_op jit(solution)/shard_map/add | solution.py:96
  (16 shorter events, 1.0 us)
Async XLA Ops:
  56.6 39.8 %copy-start.1 = (f32[7]{0:T(128)}, f32[7]{0:T(128)S(1)}, u32[]{:S(2)}) copy-start(f32[7]{0:T(128)S(1)} %broadcast_divide_fusion) | copy-start | bytes 88
  64.7 15.1 %collective-permute-start = (f32[1,32,32,3]{3,2,1,0:T(8,128)S(1)}, f32[1,32,32,3]{3,2,1,0:T(8,128)S(1)}, u32[]{:S(2)}, u32[]{:S(2)}) collective-permute-start(f32[1,32,32,3]{3,2,1,0:T(8,128)S(1)} %get-tuple-element.8), channel_id=1, source_target_pairs={{0,64},{64,128},{128,192},{192,0},{1,65},{65,129},{129,193},{193,1... | collective-permute-start | bytes 36872 | tf_op jit(solution)/shard_map/ppermute | solution.py:22
  68.3 14.9 %collective-permute-start.1 = (f32[1,32,32,3]{3,2,1,0:T(8,128)S(1)}, f32[1,32,32,3]{3,2,1,0:T(8,128)S(1)}, u32[]{:S(2)}, u32[]{:S(2)}) collective-permute-start(f32[1,32,32,3]{3,2,1,0:T(8,128)S(1)} %get-tuple-element.9), channel_id=1, source_target_pairs={{64,0},{128,64},{192,128},{0,192},{65,1},{129,65},{193,129},{1,193... | collective-permute-start | bytes 36872 | tf_op jit(solution)/shard_map/ppermute | solution.py:24
  83.2 13.2 %copy-start = (f32[7,32,32,128]{3,2,1,0:T(8,128)S(1)}, f32[7,32,32,128]{3,2,1,0:T(8,128)}, u32[]{:S(2)}) copy-start(f32[7,32,32,128]{3,2,1,0:T(8,128)} %param.2) | copy-start | bytes 11010052
  83.5 6.1 %collective-permute-start.2 = (f32[1,32,3,134]{3,2,1,0:T(4,128)S(1)}, f32[1,32,3,134]{3,2,1,0:T(4,128)S(1)}, u32[]{:S(2)}, u32[]{:S(2)}) collective-permute-start(f32[1,32,3,134]{3,2,1,0:T(4,128)S(1)} %get-tuple-element.6), channel_id=1, source_target_pairs={{0,16},{16,32},{32,48},{48,0},{1,17},{17,33},{33,49},{49,1},{2,18}... | collective-permute-start | bytes 154376 | tf_op jit(solution)/shard_map/ppermute | solution.py:22
  87.1 6.2 %collective-permute-start.3 = (f32[1,32,3,134]{3,2,1,0:T(4,128)S(1)}, f32[1,32,3,134]{3,2,1,0:T(4,128)S(1)}, u32[]{:S(2)}, u32[]{:S(2)}) collective-permute-start(f32[1,32,3,134]{3,2,1,0:T(4,128)S(1)} %get-tuple-element.7), channel_id=1, source_target_pairs={{16,0},{32,16},{48,32},{0,48},{17,1},{33,17},{49,33},{1,49},{18,2}... | collective-permute-start | bytes 154376 | tf_op jit(solution)/shard_map/ppermute | solution.py:24
  93.4 8.2 %collective-permute-start.4 = (f32[1,3,38,134]{3,2,1,0:T(8,128)S(1)}, f32[1,3,38,134]{3,2,1,0:T(8,128)S(1)}, u32[]{:S(2)}, u32[]{:S(2)}) collective-permute-start(f32[1,3,38,134]{3,2,1,0:T(8,128)S(1)} %get-tuple-element.4), channel_id=1, source_target_pairs={{0,1},{1,2},{2,3},{3,4},{4,5},{5,6},{6,7},{7,8},{8,9},{9,10},{10,1... | collective-permute-start | bytes 183320 | tf_op jit(solution)/shard_map/ppermute | solution.py:22
  93.5 8.1 %collective-permute-start.5 = (f32[1,3,38,134]{3,2,1,0:T(8,128)S(1)}, f32[1,3,38,134]{3,2,1,0:T(8,128)S(1)}, u32[]{:S(2)}, u32[]{:S(2)}) collective-permute-start(f32[1,3,38,134]{3,2,1,0:T(8,128)S(1)} %get-tuple-element.5), channel_id=1, source_target_pairs={{1,0},{2,1},{3,2},{4,3},{5,4},{6,5},{7,6},{8,7},{9,8},{10,9},{11,1... | collective-permute-start | bytes 183320 | tf_op jit(solution)/shard_map/ppermute | solution.py:24
where the time goes:
time: 109 us
  blocking collectives  37.4 us (34%)
  matrix products  28.4 us (26%)
  waiting for transfers between devices  21.1 us (19%)
  other arithmetic  11 us (10%)
  starting transfers between devices  10.1 us (9%)
    psum x4, blocking collectives, one_axis_at_a_time(): shard = lax.psum(shard, axis)  37.4 us
    dot_general x1, matrix products, on_device(): jnp.dot(flat, flat.T, precision=lax.Precision.HIGHEST, preferred_element_...  14.5 us
    ppermute x3, waiting for transfers between devices, extended(): lax.ppermute(tail, axis, [(i, (i + 1) % count) for i in range(count)])  14 us
    dot_general x1, matrix products, on_device(): jnp.tensordot(weights, residuals, axes=1, precision=lax.Precision.HIGHEST)  7.85 us
    ppermute x3, starting transfers between devices, extended(): lax.ppermute(tail, axis, [(i, (i + 1) % count) for i in range(count)])  7.18 us
    ppermute x3, waiting for transfers between devices, extended(): lax.ppermute(head, axis, [((i + 1) % count, i) for i in range(count)])  7.07 us
    dot_general x1, matrix products, on_device(): jnp.tensordot(weights, densities, axes=1, precision=lax.Precision.HIGHEST)  5.18 us
    ppermute x3, starting transfers between devices, extended(): lax.ppermute(head, axis, [((i + 1) % count, i) for i in range(count)])  2.95 us
  transfers between devices with their start and end apart: 6, of which 4 were waited for; matrix products, arithmetic and copies ran while one was open for 5% of the time, Pallas kernels for 0%

commit v1 on v0

--- a/solution.py
+++ b/solution.py
@@ -10,6 +10,7 @@
 GZ = ("gz_0", "gz_1")
 shift_value = 0.15
 mix_amount = 0.7
+enter_cells_all = lambda point, axis_tag: jnp.sum(jax.lax.all_gather(point, axis_tag), axis=0)
 
 
 def extended(cells, sides, width):
@@ -30,7 +31,7 @@
 
 def one_axis_at_a_time(shard, axes):
     for axis in axes:
-        shard = lax.psum(shard, axis)
+        shard = enter_cells_all(shard, axis)
     return shard
 
 

time: 109 us -> 122 us (1.12)
  blocking collectives: 37.4 us -> 54.3 us
  starting transfers between devices: 10.1 us -> 7.17 us
  waiting for transfers between devices: 21.1 us -> 18.6 us
    all_gather x0 -> x4, blocking collectives: none -> 54.3 us  [jax.lax.all_gather(point, axis_tag)]
    psum x4 -> x0, blocking collectives: 37.4 us -> none  [one_axis_at_a_time(): shard = lax.psum(shard, axis)]
    ppermute x3, starting transfers between devices: 7.18 us -> 1.77 us  [extended(): lax.ppermute(tail, axis, [(i, (i + 1) % count) for i in range(count)])]
    ppermute x3, waiting for transfers between devices: 7.07 us -> 3.74 us  [extended(): lax.ppermute(head, axis, [((i + 1) % count, i) for i in range(count)])]
    ppermute x3, starting transfers between devices: 2.95 us -> 5.4 us  [extended(): lax.ppermute(head, axis, [((i + 1) % count, i) for i in range(count)])]
  transfers between devices with their start and end apart: 6 -> 6, of which waited for: 4 -> 4; matrix products, arithmetic and copies ran while one was open for 5% -> 4% of each run, Pallas kernels for 0% -> 0%
where the time goes in v1:
time: 122 us
  blocking collectives  54.3 us (45%)
  matrix products  29.4 us (24%)
  waiting for transfers between devices  18.6 us (15%)
  other arithmetic  11 us (9%)
  starting transfers between devices  7.17 us (6%)
    all_gather x4, blocking collectives, jax.lax.all_gather(point, axis_tag)  54.3 us
    dot_general x1, matrix products, on_device(): jnp.dot(flat, flat.T, precision=lax.Precision.HIGHEST, preferred_element_...  15.5 us
    ppermute x3, waiting for transfers between devices, extended(): lax.ppermute(tail, axis, [(i, (i + 1) % count) for i in range(count)])  14.9 us
    dot_general x1, matrix products, on_device(): jnp.tensordot(weights, residuals, axes=1, precision=lax.Precision.HIGHEST)  7.85 us
    ppermute x3, starting transfers between devices, extended(): lax.ppermute(head, axis, [((i + 1) % count, i) for i in range(count)])  5.4 us
    dot_general x1, matrix products, on_device(): jnp.tensordot(weights, densities, axes=1, precision=lax.Precision.HIGHEST)  5.18 us
    ppermute x3, waiting for transfers between devices, extended(): lax.ppermute(head, axis, [((i + 1) % count, i) for i in range(count)])  3.74 us
    add x1, other arithmetic, relax(): centre + omega * (rhs - diag_value * centre + neighbours(padded)) / diag_...  2.59 us
  transfers between devices with their start and end apart: 6, of which 4 were waited for; matrix products, arithmetic and copies ran while one was open for 4% of the time, Pallas kernels for 0%

profile of v1, /device:TPU:30, one launch (start us, length us, event | category | flops | bytes accessed | tf_op | source)
XLA Modules:
  0.0 121.6 jit_solution(17874397126142215052)
XLA Ops:
  0.6 15.5 %fusion.10 = f32[1,7,7]{2,1,0:T(8,128)S(1)} fusion(f32[7,32,32,128]{3,2,1,0:T(8,128)} %param.3), kind=kOutput, calls=%fused_computation.23 | convolution fusion | flops 77070336 | bytes 3670212 | tf_op jit(solution)/shard_map/dot_general | solution.py:83
  16.1 12.0 %all-gather.4 = f32[4,7,7]{2,1,0:T(8,128)S(1)} all-gather(f32[1,7,7]{2,1,0:T(8,128)S(1)} %fusion.10), channel_id=2, replica_groups=mesh['gx'=4,'gy'=4,'gz_0'=8,'gz_1'=2] {'gx'}, dimensions={0}, use_global_device_ids=true | all-gather | bytes 980 | tf_op jit(solution)/shard_map/all_gather | solution.py:13
  28.1 12.0 %all-gather.5 = f32[4,7,7]{2,1,0:T(8,128)S(1)} all-gather(f32[1,7,7]{2,1,0:T(8,128)S(1)} %bitcast.54), channel_id=3, replica_groups=mesh['gx'=4,'gy'=4,'gz_0'=8,'gz_1'=2] {'gy'}, dimensions={0}, use_global_device_ids=true | all-gather | bytes 980 | tf_op jit(solution)/shard_map/all_gather | solution.py:13
  40.2 28.3 %all-gather.6 = f32[8,7,7]{2,1,0:T(8,128)S(1)} all-gather(f32[1,7,7]{2,1,0:T(8,128)S(1)} %bitcast.55), channel_id=4, replica_groups=mesh['gx'=4,'gy'=4,'gz_0'=8,'gz_1'=2] {'gz_0'}, dimensions={0}, use_global_device_ids=true | all-gather | bytes 1764 | tf_op jit(solution)/shard_map/all_gather | solution.py:13
  68.4 2.0 %all-gather.7 = f32[2,7,7]{2,1,0:T(8,128)S(1)} all-gather(f32[1,7,7]{2,1,0:T(8,128)S(1)} %bitcast.53), channel_id=5, replica_groups=mesh['gx'=4,'gy'=4,'gz_0'=8,'gz_1'=2] {'gz_1'}, dimensions={0}, use_global_device_ids=true | all-gather | bytes 588 | tf_op jit(solution)/shard_map/all_gather | solution.py:13
  71.2 0.6 compare_reduce_fusion
  71.9 0.6 fusion.19
  73.2 0.8 fusion.29
  73.9 0.6 broadcast_divide_fusion
  74.6 7.8 %fusion = f32[1,32,32,128]{3,0,2,1:T(1,128)S(1)} fusion(f32[7,32,32,128]{3,2,1,0:T(8,128)} %param.3, f32[7]{0:T(128)S(1)} %broadcast_divide_fusion), kind=kOutput, calls=%fused_computation | convolution fusion | flops 11010048 | bytes 4194332 | tf_op jit(solution)/shard_map/dot_general | solution.py:95
  82.7 0.9 collective-permute-start
  83.6 1.2 collective-permute-start.1
  84.8 12.0 %collective-permute-done = f32[1,32,32,3]{3,2,1,0:T(8,128)S(1)} collective-permute-done((f32[1,32,32,3]{3,2,1,0:T(8,128)S(1)}, f32[1,32,32,3]{3,2,1,0:T(8,128)S(1)}, u32[]{:S(2)}, u32[]{:S(2)}) %collective-permute-start) | collective-permute-done | bytes 12320 | tf_op jit(solution)/shard_map/ppermute | solution.py:23
  96.7 1.8 %collective-permute-done.1 = f32[1,32,32,3]{3,2,1,0:T(8,128)S(1)} collective-permute-done((f32[1,32,32,3]{3,2,1,0:T(8,128)S(1)}, f32[1,32,32,3]{3,2,1,0:T(8,128)S(1)}, u32[]{:S(2)}, u32[]{:S(2)}) %collective-permute-start.1) | collective-permute-done | bytes 12320 | tf_op jit(solution)/shard_map/ppermute | solution.py:25
  98.8 0.8 collective-permute-start.2
  99.6 1.3 %collective-permute-start.3 = (f32[1,32,3,134]{3,2,1,0:T(4,128)S(1)}, f32[1,32,3,134]{3,2,1,0:T(4,128)S(1)}, u32[]{:S(2)}, u32[]{:S(2)}) collective-permute-start(f32[1,32,3,134]{3,2,1,0:T(4,128)S(1)} %get-tuple-element.7), channel_id=1, source_target_pairs={{16,0},{32,16},{48,32},{0,48},{17,1},{33,17},{49,33},{1,49},{18,2}... | collective-permute-start | bytes 154376 | tf_op jit(solution)/shard_map/ppermute | solution.py:25
  100.9 2.9 %collective-permute-done.2 = f32[1,32,3,134]{3,2,1,0:T(4,128)S(1)} collective-permute-done((f32[1,32,3,134]{3,2,1,0:T(4,128)S(1)}, f32[1,32,3,134]{3,2,1,0:T(4,128)S(1)}, u32[]{:S(2)}, u32[]{:S(2)}) %collective-permute-start.2) | collective-permute-done | bytes 51488 | tf_op jit(solution)/shard_map/ppermute | solution.py:23
  103.8 2.0 %collective-permute-done.3 = f32[1,32,3,134]{3,2,1,0:T(4,128)S(1)} collective-permute-done((f32[1,32,3,134]{3,2,1,0:T(4,128)S(1)}, f32[1,32,3,134]{3,2,1,0:T(4,128)S(1)}, u32[]{:S(2)}, u32[]{:S(2)}) %collective-permute-start.3) | collective-permute-done | bytes 51488 | tf_op jit(solution)/shard_map/ppermute | solution.py:25
  106.0 2.9 %collective-permute-start.5 = (f32[1,3,38,134]{3,2,1,0:T(8,128)S(1)}, f32[1,3,38,134]{3,2,1,0:T(8,128)S(1)}, u32[]{:S(2)}, u32[]{:S(2)}) collective-permute-start(f32[1,3,38,134]{3,2,1,0:T(8,128)S(1)} %get-tuple-element.5), channel_id=1, source_target_pairs={{1,0},{2,1},{3,2},{4,3},{5,4},{6,5},{7,6},{8,7},{9,8},{10,9},{11,1... | collective-permute-start | bytes 183320 | tf_op jit(solution)/shard_map/ppermute | solution.py:25
  108.9 5.2 %fusion.4 = f32[1,32,32,128]{3,0,2,1:T(1,128)S(1)} fusion(f32[7,32,32,128]{3,2,1,0:T(8,128)S(1)} %copy-done, f32[7]{0:T(128)S(1)} %broadcast_divide_fusion), kind=kOutput, calls=%fused_computation.4 | convolution fusion | flops 11010048 | bytes 4194332 | tf_op jit(solution)/shard_map/dot_general | solution.py:94
  114.2 0.6 pad_maximum_fusion
  114.8 2.3 %broadcast_multiply_fusion = (f32[1,36,36,132]{3,2,1,0:T(8,128)S(1)}, f32[1,36,36,132]{3,2,1,0:T(8,128)S(1)}) fusion(f32[1,38,38,134]{3,2,1,0:T(8,128)S(1)} %pad_maximum_fusion), kind=kLoop, calls=%fused_computation.26 | loop fusion | flops 1368576 | bytes 6158592 | tf_op jit(solution)/shard_map/div | solution.py:73
  117.1 2.6 %fusion.9 = f32[1,34,34,130]{3,2,1,0:T(8,128)S(1)} fusion(f32[1,36,36,132]{3,2,1,0:T(8,128)S(1)} %get-tuple-element.2, f32[1,36,36,132]{3,2,1,0:T(8,128)S(1)} %get-tuple-element.3), kind=kLoop, calls=%fused_computation.17 | loop fusion | flops 1502800 | bytes 5410080 | tf_op jit(solution)/shard_map/add | solution.py:65
  119.7 1.8 %fusion.18 = f32[32,32,128]{2,1,0:T(8,128)} fusion(f32[32,32,128]{2,1,0:T(8,128)S(1)} %bitcast.52, f32[1,34,34,130]{3,2,1,0:T(8,128)S(1)} %fusion.9, f32[1,36,36,132]{3,2,1,0:T(8,128)S(1)} %get-tuple-element.3), kind=kLoop, calls=%fused_computation.33 | loop fusion | flops 1572864 | bytes 5242880 | tf_op jit(solution)/shard_map/add | solution.py:97
  (20 shorter events, 2.1 us)
Async XLA Ops:
  74.6 34.3 %copy-start.1 = (f32[7]{0:T(128)}, f32[7]{0:T(128)S(1)}, u32[]{:S(2)}) copy-start(f32[7]{0:T(128)S(1)} %broadcast_divide_fusion) | copy-start | bytes 88
  82.7 14.1 %collective-permute-start = (f32[1,32,32,3]{3,2,1,0:T(8,128)S(1)}, f32[1,32,32,3]{3,2,1,0:T(8,128)S(1)}, u32[]{:S(2)}, u32[]{:S(2)}) collective-permute-start(f32[1,32,32,3]{3,2,1,0:T(8,128)S(1)} %get-tuple-element.8), channel_id=1, source_target_pairs={{0,64},{64,128},{128,192},{192,0},{1,65},{65,129},{129,193},{193,1... | collective-permute-start | bytes 36872 | tf_op jit(solution)/shard_map/ppermute | solution.py:23
  83.6 14.9 %collective-permute-start.1 = (f32[1,32,32,3]{3,2,1,0:T(8,128)S(1)}, f32[1,32,32,3]{3,2,1,0:T(8,128)S(1)}, u32[]{:S(2)}, u32[]{:S(2)}) collective-permute-start(f32[1,32,32,3]{3,2,1,0:T(8,128)S(1)} %get-tuple-element.9), channel_id=1, source_target_pairs={{64,0},{128,64},{192,128},{0,192},{65,1},{129,65},{193,129},{1,193... | collective-permute-start | bytes 36872 | tf_op jit(solution)/shard_map/ppermute | solution.py:25
  98.5 10.4 %copy-start = (f32[7,32,32,128]{3,2,1,0:T(8,128)S(1)}, f32[7,32,32,128]{3,2,1,0:T(8,128)}, u32[]{:S(2)}) copy-start(f32[7,32,32,128]{3,2,1,0:T(8,128)} %param.2) | copy-start | bytes 11010052
  98.8 5.0 %collective-permute-start.2 = (f32[1,32,3,134]{3,2,1,0:T(4,128)S(1)}, f32[1,32,3,134]{3,2,1,0:T(4,128)S(1)}, u32[]{:S(2)}, u32[]{:S(2)}) collective-permute-start(f32[1,32,3,134]{3,2,1,0:T(4,128)S(1)} %get-tuple-element.6), channel_id=1, source_target_pairs={{0,16},{16,32},{32,48},{48,0},{1,17},{17,33},{33,49},{49,1},{2,18}... | collective-permute-start | bytes 154376 | tf_op jit(solution)/shard_map/ppermute | solution.py:23
  99.6 6.2 %collective-permute-start.3 = (f32[1,32,3,134]{3,2,1,0:T(4,128)S(1)}, f32[1,32,3,134]{3,2,1,0:T(4,128)S(1)}, u32[]{:S(2)}, u32[]{:S(2)}) collective-permute-start(f32[1,32,3,134]{3,2,1,0:T(4,128)S(1)} %get-tuple-element.7), channel_id=1, source_target_pairs={{16,0},{32,16},{48,32},{0,48},{17,1},{33,17},{49,33},{1,49},{18,2}... | collective-permute-start | bytes 154376 | tf_op jit(solution)/shard_map/ppermute | solution.py:25
  106.0 8.2 %collective-permute-start.4 = (f32[1,3,38,134]{3,2,1,0:T(8,128)S(1)}, f32[1,3,38,134]{3,2,1,0:T(8,128)S(1)}, u32[]{:S(2)}, u32[]{:S(2)}) collective-permute-start(f32[1,3,38,134]{3,2,1,0:T(8,128)S(1)} %get-tuple-element.4), channel_id=1, source_target_pairs={{0,1},{1,2},{2,3},{3,4},{4,5},{5,6},{6,7},{7,8},{8,9},{9,10},{10,1... | collective-permute-start | bytes 183320 | tf_op jit(solution)/shard_map/ppermute | solution.py:23
  106.0 8.1 %collective-permute-start.5 = (f32[1,3,38,134]{3,2,1,0:T(8,128)S(1)}, f32[1,3,38,134]{3,2,1,0:T(8,128)S(1)}, u32[]{:S(2)}, u32[]{:S(2)}) collective-permute-start(f32[1,3,38,134]{3,2,1,0:T(8,128)S(1)} %get-tuple-element.5), channel_id=1, source_target_pairs={{1,0},{2,1},{3,2},{4,3},{5,4},{6,5},{7,6},{8,7},{9,8},{10,9},{11,1... | collective-permute-start | bytes 183320 | tf_op jit(solution)/shard_map/ppermute | solution.py:25
